TPU v7x, 256 devices: a whole 4x4x8 slice. The times are simulated.
256 devices in a mesh: slab: 128 (over z, x, y), head: 2 (over core).
Axes of the slice: x: 4, y: 4, z: 8, core: 2. Of those that a mesh axis runs over, the one named last changes fastest.
Arguments:
- directions: bfloat16 [2, 32768, 5120], P(None, 'slab', 'head'), may hold values from -0.59765625 to 0.59765625
- magnitudes: float32 [4, 40, 32768], P(None, 'head', 'slab'), may hold values from 4 to 24
- outlier_rows: bfloat16 [16384, 4, 5120], P('slab', None, 'head'), may hold values from -6 to 6
- outlier_counts: int32 [128], P('slab'), may hold values from 64 to 128
- destinations: int32 [16384, 1], P('slab'), may hold values from 0 to 127; in each aligned block of 128 rows (0 to 127, 128 to 255, ...) at most 2 rows name the same one
- retention_order: int32 [128, 256], P('slab'), may hold values from 0 to 255, each once within a row
Outputs:
- restored: bfloat16 [4, 32768, 5120], P(None, 'slab', 'head')
Inputs may be any that keep to these rules, and one draw needn't show every extreme that they name: `outlier_counts`: at least 64 rows of each slab are live. `destinations`: among the 128 rows of one slab at most 2 name the same destination slab. `retention_order`: each slab's row is a permutation of its token positions.
All inputs are finite; a program needn't handle non-finite values.
Results may differ from a plain program's by a relative error of at most 0.0013.
Values may be sent and summed in bfloat16 or wider, within the bound.
No kernel may reach another device: no remote copies, remote signals or barrier semaphores. Data moves between devices by JAX's collectives and lax.ppermute only.
A program may use at most 128 MiB of HBM per device.

v0:
```python
import jax
import jax.numpy as jnp
from jax import lax
from jax.sharding import Mesh
from jax.sharding import PartitionSpec as P

SLAB = ("slab_0", "slab_1", "slab_2")


def filled_with(shard, identity):
    return jnp.broadcast_to(jnp.asarray(identity, shard.dtype), shard.shape)


def carried_in(shard, axes, combine, identity):
    before = start = filled_with(shard, identity)
    running = shard
    for axis in reversed(axes):
        devices, mine = (lax.axis_size(axis), lax.axis_index(axis))
        pieces = lax.all_gather(running, axis)
        inside, running = (start, start)
        for k in range(devices):
            passed = k < mine
            running = combine(running, pieces[k])
            inside = jnp.where(passed, running, inside)
        before = combine(inside, before)
    return before


def passed_along(block, axis, distance):
    devices = range(lax.axis_size(axis))
    route = [((i - distance) % len(devices), i) for i in devices]
    return lax.ppermute(block, axis, route)


def add_counts(earlier, later):
    return earlier + later


def per_device(directions, magnitudes, outlier_rows, outlier_counts, destinations, retention_order):
    slab_count = lax.axis_size(SLAB)
    tok_rows = directions.shape[1]
    row_slots = outlier_rows.shape[0]
    features = outlier_rows.shape[2]
    heads_here = magnitudes.shape[1]
    head_size = features // heads_here
    pair_cap = max(2, tok_rows // slab_count)
    total_slots = slab_count * pair_cap
    target = destinations[:, 0]
    active = jnp.arange(row_slots, dtype=jnp.int32) < outlier_counts[0]
    columns = jnp.arange(slab_count, dtype=jnp.int32)
    chosen = ((target[:, None] == columns[None, :]) & active[:, None]).astype(jnp.int32)
    pair_counts = jnp.sum(chosen, axis=0)
    offsets = carried_in(pair_counts, SLAB, add_counts, jnp.zeros_like(pair_counts))
    within = jnp.sum(chosen * (jnp.cumsum(chosen, axis=0) - 1), axis=1)
    arrival = jnp.sum(chosen * offsets[None, :], axis=1) + within
    slot_number = target * pair_cap + within
    picker = (jnp.arange(total_slots, dtype=jnp.int32)[:, None] == slot_number[None, :]) & active[
        None, :
    ]
    packed = jnp.dot(
        picker.astype(jnp.bfloat16),
        outlier_rows.reshape(row_slots, 4 * features),
        preferred_element_type=jnp.float32,
    ).astype(jnp.bfloat16)
    packed_arrival = jnp.sum(picker.astype(jnp.int32) * (arrival + 1)[None, :], axis=1) - 1
    packed = packed.reshape(slab_count, pair_cap, 4 * features)
    packed_arrival = packed_arrival.reshape(slab_count, pair_cap)
    edges = (
        passed_along(directions[:, 0:1, :], SLAB, -1),
        passed_along(magnitudes[:, :, 0:1].astype(jnp.bfloat16), SLAB, -1).astype(jnp.float32),
    )
    token_dirs = jnp.concatenate([directions[:, 1:, :], edges[0]], axis=1)
    token_mags = jnp.concatenate([magnitudes[:, :, 1:], edges[1]], axis=2)
    factor = jnp.transpose(token_mags, (0, 2, 1)).reshape(2, 2, tok_rows, heads_here, 1)
    scaled = factor * token_dirs.reshape(1, 2, tok_rows, heads_here, head_size)
    scaled = scaled.reshape(4, tok_rows, features).astype(jnp.bfloat16)
    arrived, arrived_number = (
        lax.all_to_all(packed, SLAB, split_axis=0, concat_axis=0, tiled=True),
        lax.all_to_all(packed_arrival, SLAB, split_axis=0, concat_axis=0, tiled=True),
    )
    arrived = arrived.reshape(total_slots, 4, features)
    arrived_number = arrived_number.reshape(total_slots)
    sequence = retention_order[0]
    token_positions = jnp.arange(tok_rows, dtype=jnp.int32)
    landing = jnp.sum(
        jnp.where(arrived_number[:, None] == token_positions[None, :], sequence[None, :], 0), axis=1
    )
    filled = arrived_number >= 0
    placer = ((token_positions[:, None] == landing[None, :]) & filled[None, :]).astype(jnp.bfloat16)
    inserted = jnp.einsum(
        "tj,jkf->ktf", placer, arrived, preferred_element_type=jnp.float32
    ).astype(jnp.bfloat16)
    covered = jnp.sum(placer.astype(jnp.float32), axis=1) > 0.5
    return jnp.where(covered[None, :, None], inserted, scaled)


def solution(mesh):
    finer = Mesh(
        mesh.devices.reshape(8, 4, 4, mesh.shape["head"]), ("slab_0", "slab_1", "slab_2", "head")
    )
    placed = (
        P(None, SLAB, "head"),
        P(None, "head", SLAB),
        P(SLAB, None, "head"),
        P(SLAB),
        P(SLAB, None),
        P(SLAB, None),
    )
    return jax.shard_map(
        per_device, mesh=finer, in_specs=placed, out_specs=P(None, SLAB, "head"), check_vma=False
    )
```

profile of v0, /device:TPU:30, one launch (start us, length us, event | category | flops | bytes accessed | tf_op | source)
XLA Modules:
  0.0 224.5 jit_solution(5345941299234713863)
XLA Ops:
  0.7 0.8 fusion.13
  1.4 0.8 fusion.15
  2.2 0.2 reduce_window_sum.11
  2.4 6.7 %all-gather.1 = s32[4,1,128]{2,1,0:T(1,128)S(1)} all-gather(s32[1,1,128]{2,1,0:T(1,128)S(1)} %bitcast.68), channel_id=2, replica_groups=mesh['slab_0'=8,'slab_1'=4,'slab_2'=4,'head'=2] {'slab_2'}, dimensions={0}, use_global_device_ids=true | all-gather | bytes 2560 | tf_op jit(solution)/shard_map/all_gather | solution.py:19
  9.1 7.2 %all-gather.2 = s32[4,1,128]{2,1,0:T(1,128)S(1)} all-gather(s32[1,1,128]{2,1,0:T(1,128)S(1)} %slice_add_fusion.6), channel_id=1, replica_groups=mesh['slab_0'=8,'slab_1'=4,'slab_2'=4,'head'=2] {'slab_1'}, dimensions={0}, use_global_device_ids=true | all-gather | bytes 2560 | tf_op jit(solution)/shard_map/all_gather | solution.py:19
  16.3 18.6 %all-gather.3 = s32[8,1,128]{2,1,0:T(1,128)S(1)} all-gather(s32[1,1,128]{2,1,0:T(1,128)S(1)} %slice_add_fusion.3), channel_id=1, replica_groups=mesh['slab_0'=8,'slab_1'=4,'slab_2'=4,'head'=2] {'slab_0'}, dimensions={0}, use_global_device_ids=true | all-gather | bytes 4608 | tf_op jit(solution)/shard_map/all_gather | solution.py:19
  35.0 0.8 select_reduce_fusion.3
  35.8 0.7 multiply_add_fusion
  36.5 0.1 select_reduce_fusion.1
  36.6 0.8 sub.12
  37.4 12.0 %all-to-all-start = ((s32[128,1,2]{2,1,0:T(1,128)}), s32[128,1,2]{2,1,0:T(1,128)S(1)}, u32[]{:S(2)}, u32[]{:S(2)}) async-start(s32[128,1,2]{2,1,0:T(1,128)} %bitcast.15), calls=%async_computation | async-start | bytes 131072 | tf_op jit(solution)/shard_map/all_to_all | solution.py:79
  49.3 2.2 copy.33
  51.6 3.9 %convolution_convert_fusion = bf16[256,10240]{1,0:T(8,128)(2,1)} fusion(bf16[128,10240]{1,0:T(8,128)(2,1)S(1)} %bitcast.59, s32[128]{0:T(128)S(1)} %get-tuple-element.7, pred[128]{0:T(512)(128)(4,1)S(1)} %iota_compare_fusion.4), kind=kOutput, calls=%fused_computation | convolution fusion | flops 673775616 | bytes 7864960 | tf_op jit(solution)/shard_map/dot_general | solution.py:60
  55.5 8.3 %reshape.78 = bf16[128,2,10240]{2,1,0:T(2,128)(2,1)} reshape(bf16[256,10240]{1,0:T(8,128)(2,1)} %convolution_convert_fusion) | data formatting | bytes 10485760 | tf_op jit(solution)/shard_map/reshape | solution.py:66
  63.8 0.0 copy-start
  63.8 0.0 copy-start.1
  63.8 0.0 all-to-all-done
  63.8 14.3 %all-to-all-start.1 = ((bf16[128,2,10240]{2,1,0:T(2,128)(2,1)}), bf16[128,2,10240]{2,1,0:T(2,128)(2,1)}, u32[]{:S(2)}, u32[]{:S(2)}) async-start(bf16[128,2,10240]{2,1,0:T(2,128)(2,1)} %reshape.78), calls=%async_computation.1 | async-start | bytes 10485760 | tf_op jit(solution)/shard_map/all_to_all | solution.py:78
  78.1 0.0 copy-done
  78.2 0.9 collective-permute-start.1
  79.1 0.0 copy-done.1
  79.1 0.0 copy-start.2
  79.1 0.8 collective-permute-start
  79.9 2.1 slice.79
  82.0 0.1 slice.77
  82.1 3.0 %copy.31 = bf16[2,255,2560]{1,2,0:T(8,128)(2,1)S(1)} copy(bf16[2,255,2560]{2,1,0:T(8,128)(2,1)} %slice.79) | data formatting | bytes 5222400
  85.1 98.4 %collective-permute-done = bf16[4,20,1]{2,0,1:T(4,128)(2,1)S(1)} collective-permute-done((bf16[4,20,1]{2,0,1:T(4,128)(2,1)S(1)}, bf16[4,20,1]{2,0,1:T(4,128)(2,1)S(1)}, u32[]{:S(2)}, u32[]{:S(2)}) %collective-permute-start) | collective-permute-done | bytes 192 | tf_op jit(solution)/shard_map/ppermute | solution.py:32
  183.5 0.1 maximum_bitcast_fusion
  183.6 0.5 broadcast.165
  184.1 0.8 reduce.3
  184.9 0.1 eq.61
  185.1 0.0 copy-done.2
  185.1 0.2 select_reduce_fusion
  185.3 0.1 convert_reduce_fusion
  185.4 0.0 collective-permute-done.1
  185.4 1.5 copy.28
  187.0 2.1 pad_maximum_fusion
  189.1 0.7 convert.5
  189.8 4.3 %multiply_convert_fusion = bf16[2,2,256,20,128]{2,4,3,1,0:T(8,128)(2,1)} fusion(f32[2,256,20,128]{1,3,2,0:T(8,128)S(1)} %convert.5, f32[2,2,256,20]{2,3,1,0:T(8,128)S(1)} %bitcast.63), kind=kLoop, calls=%fused_computation.1 | loop fusion | flops 5242880 | bytes 10567680 | tf_op jit(solution)/shard_map/convert_element_type | solution.py:76
  194.0 0.0 all-to-all-done.1
  194.0 13.4 %reshape.79 = bf16[256,4,2560]{2,1,0:T(4,128)(2,1)} reshape(bf16[128,2,10240]{2,1,0:T(2,128)(2,1)} %all-to-all-done.1) | data formatting | bytes 10485760 | tf_op jit(solution)/shard_map/reshape | solution.py:81
  207.4 9.1 %bitcast_select_fusion = bf16[4,256,2560]{1,2,0:T(8,128)(2,1)} fusion(bf16[4,256,2560]{1,2,0:T(8,128)(2,1)} %bitcast.61, pred[256]{0:T(512)(128)(4,1)S(1)} %broadcast_compare_fusion, bf16[256,4,2560]{2,1,0:T(4,128)(2,1)} %reshape.79, s32[256]{0:T(256)S(1)} %select_reduce_fusion, pred[256]{0:T(512)(128)(4,1)S(1)} %broadcast_compare_fusion.1), kind=kOutput, calls=%fused_computation.3 | convolution fusion | flops 1347551232 | bytes 15730176 | tf_op jit(solution)/shard_map/tj,jkf->ktf/dot_general | solution.py:90
  216.6 7.9 %copy.29 = bf16[4,256,2560]{2,1,0:T(8,128)(2,1)} copy(bf16[4,256,2560]{1,2,0:T(8,128)(2,1)} %bitcast_select_fusion) | data formatting | bytes 10485760 | tf_op jit(solution)/shard_map/jit(_where)/select_n | solution.py:94
  (12 shorter events, 0.1 us)
Async XLA Ops:
  37.4 26.4 %all-to-all-start = ((s32[128,1,2]{2,1,0:T(1,128)}), s32[128,1,2]{2,1,0:T(1,128)S(1)}, u32[]{:S(2)}, u32[]{:S(2)}) async-start(s32[128,1,2]{2,1,0:T(1,128)} %bitcast.15), calls=%async_computation | async-start | bytes 131072 | tf_op jit(solution)/shard_map/all_to_all | solution.py:79
  63.8 14.3 %copy-start = (bf16[2,256,2560]{2,1,0:T(8,128)(2,1)S(1)}, bf16[2,256,2560]{2,1,0:T(8,128)(2,1)}, u32[]{:S(2)}) copy-start(bf16[2,256,2560]{2,1,0:T(8,128)(2,1)} %param.6) | copy-start | bytes 7864324
  63.8 15.3 %copy-start.1 = (f32[4,20,256]{2,0,1:T(4,128)S(1)}, f32[4,20,256]{2,0,1:T(4,128)}, u32[]{:S(2)}) copy-start(f32[4,20,256]{2,0,1:T(4,128)} %param.7) | copy-start | bytes 245764
  63.8 130.2 %all-to-all-start.1 = ((bf16[128,2,10240]{2,1,0:T(2,128)(2,1)}), bf16[128,2,10240]{2,1,0:T(2,128)(2,1)}, u32[]{:S(2)}, u32[]{:S(2)}) async-start(bf16[128,2,10240]{2,1,0:T(2,128)(2,1)} %reshape.78), calls=%async_computation.1 | async-start | bytes 10485760 | tf_op jit(solution)/shard_map/all_to_all | solution.py:78
  78.2 107.3 %collective-permute-start.1 = (bf16[2,1,2560]{2,0,1:T(2,128)(2,1)S(1)}, bf16[2,1,2560]{2,0,1:T(2,128)(2,1)S(1)}, u32[]{:S(2)}, u32[]{:S(2)}) collective-permute-start(bf16[2,1,2560]{2,0,1:T(2,128)(2,1)S(1)} %copy.32), channel_id=1, source_target_pairs={{2,0},{4,2},{6,4},{8,6},{10,8},{12,10},{14,12},{16,14},{18,16},{20... | collective-permute-start | bytes 30728 | tf_op jit(solution)/shard_map/ppermute | solution.py:32
  79.1 106.0 %copy-start.2 = (s32[1,256]{1,0:T(1,128)S(1)}, s32[1,256]{1,0:T(1,128)}, u32[]{:S(2)}) copy-start(s32[1,256]{1,0:T(1,128)} %param.11) | copy-start | bytes 3076
  79.1 104.4 %collective-permute-start = (bf16[4,20,1]{2,0,1:T(4,128)(2,1)S(1)}, bf16[4,20,1]{2,0,1:T(4,128)(2,1)S(1)}, u32[]{:S(2)}, u32[]{:S(2)}) collective-permute-start(bf16[4,20,1]{2,0,1:T(4,128)(2,1)S(1)} %slice.179), channel_id=1, source_target_pairs={{2,0},{4,2},{6,4},{8,6},{10,8},{12,10},{14,12},{16,14},{18,16},{20... | collective-permute-start | bytes 488 | tf_op jit(solution)/shard_map/ppermute | solution.py:32
where the time goes:
time: 226 us; the launch traced here: 224 us
  waiting for transfers between devices  98.4 us (44%)
  local copies, waits for them, and re-layouts  40.1 us (18%)
  blocking collectives  32.6 us (14%)
  starting transfers between devices  28 us (12%)
  matrix products  13 us (6%)
  other arithmetic  11.6 us (5%)
    ppermute x2, waiting for transfers between devices, passed_along(): return lax.ppermute(block, axis, route)  98.4 us
    all_gather x3, blocking collectives, carried_in(): pieces = lax.all_gather(running, axis)  32.6 us
    all_to_all x1, starting transfers between devices, per_device(): lax.all_to_all(packed, SLAB, split_axis=0, concat_axis=0, tiled=True)  14.3 us
    reshape x1, local copies, waits for them, and re-layouts, per_device(): arrived = arrived.reshape(total_slots, 4, features)  13.4 us
    all_to_all x1, starting transfers between devices, per_device(): lax.all_to_all(packed_arrival, SLAB, split_axis=0, concat_axis=0, tiled=T...  12 us
    dot_general x1, matrix products, per_device(): jnp.einsum('tj,jkf->ktf', placer, arrived, preferred_element_type=jnp.flo...  9.12 us
    reshape x1, local copies, waits for them, and re-layouts, per_device(): packed = packed.reshape(slab_count, pair_cap, 4 * features)  8.33 us
    select_n x1, local copies, waits for them, and re-layouts, per_device(): return jnp.where(covered[None, :, None], inserted, scaled)  7.94 us
  transfers between devices with their start and end apart: 4, of which 1 were waited for; matrix products, arithmetic and copies ran while one was open for 13% of the time, Pallas kernels for 0%

commit v1 on v0

v1 whole, which is shorter than its diff:
```python
import jax
import jax.numpy as jnp
from jax import lax
from jax.experimental import pallas as pl
from jax.experimental.pallas import tpu as pltpu
from jax.sharding import Mesh
from jax.sharding import PartitionSpec as P

SLAB = ("slab_0", "slab_1", "slab_2")
EMPTY = 2.0**127


def pack_kernel(pair_cap, dest_ref, count_ref, rows_ref, out_ref, seen, sem):
    slabs = seen.shape[0]
    slots = out_ref.shape[0]
    step = 16

    def fill(i, carry):
        out_ref[pl.ds(i * step, step)] = jnp.full((step,) + out_ref.shape[1:], EMPTY, out_ref.dtype)
        return carry

    lax.fori_loop(0, slots // step, fill, 0)

    def clear(i, carry):
        seen[i] = 0
        return carry

    lax.fori_loop(0, slabs, clear, 0, unroll=8)
    live = count_ref[0]

    def send(r, carry):
        d = dest_ref[r]
        j = seen[d]
        seen[d] = j + 1
        pltpu.make_async_copy(rows_ref.at[r], out_ref.at[d * pair_cap + j], sem).start()
        return carry

    lax.fori_loop(0, live, send, 0)

    def finish(r, carry):
        pltpu.make_async_copy(rows_ref.at[0], out_ref.at[0], sem).wait()
        return carry

    lax.fori_loop(0, live, finish, 0)


def pack(outlier_rows, destinations, outlier_counts, slab_count, pair_cap):
    row_slots, kinds, features = outlier_rows.shape
    smem = pl.BlockSpec(memory_space=pltpu.SMEM)
    return pl.pallas_call(
        lambda *refs: pack_kernel(pair_cap, *refs),
        name="pack",
        in_specs=[smem, smem, pl.BlockSpec(memory_space=pl.ANY)],
        out_specs=pl.BlockSpec(memory_space=pltpu.VMEM),
        out_shape=jax.ShapeDtypeStruct((slab_count * pair_cap, kinds, features), outlier_rows.dtype),
        scratch_shapes=[pltpu.SMEM((slab_count,), jnp.int32), pltpu.SemaphoreType.DMA],
        cost_estimate=pl.CostEstimate(
            flops=0, bytes_accessed=3 * row_slots * kinds * features * 2, transcendentals=0
        ),
    )(destinations[:, 0], outlier_counts, outlier_rows)


def scale_kernel(dirs_ref, mags_ref, out_ref):
    tokens, width = dirs_ref.shape[1], dirs_ref.shape[2]
    head_size = 128
    heads = mags_ref.shape[1]
    col0 = pl.program_id(0) * (width // head_size)
    for v in range(2):
        ahead = pltpu.roll(dirs_ref[v].astype(jnp.float32), tokens - 1, 0)
        for k in (v, v + 2):
            for c in range(width // head_size):
                out_ref[k, :, c * head_size : (c + 1) * head_size] = (
                    mags_ref[k, c] * ahead[:, c * head_size : (c + 1) * head_size]
                ).astype(out_ref.dtype)


def scale(directions, factors):
    _, tokens, features = directions.shape
    heads_per = 2
    width = heads_per * 128
    return pl.pallas_call(
        scale_kernel,
        name="scale",
        grid=(features // width,),
        in_specs=[
            pl.BlockSpec((2, tokens, width), lambda i: (0, 0, i)),
            pl.BlockSpec((4, heads_per, tokens, 1), lambda i: (0, i, 0, 0)),
        ],
        out_specs=pl.BlockSpec((4, tokens, width), lambda i: (0, 0, i)),
        out_shape=jax.ShapeDtypeStruct((4, tokens, features), directions.dtype),
        cost_estimate=pl.CostEstimate(
            flops=20 * tokens * features, bytes_accessed=12 * tokens * features, transcendentals=0
        ),
    )(directions, factors)


def place_kernel(arrived_ref, rank_ref, edge_ref, scaled_ref, out_ref, placer, covered):
    slots, kinds, width = arrived_ref.shape
    tokens = out_ref.shape[1]
    total = slots * kinds
    rows = arrived_ref[...].reshape(total, width)

    @pl.when(pl.program_id(0) == 0)
    def _():
        first = rows[:, 0:128].astype(jnp.float32)
        kind_of = lax.broadcasted_iota(jnp.int32, (total, 128), 0) % kinds
        full = jnp.where((kind_of == 0) & (first < EMPTY), 1.0, 0.0).astype(jnp.bfloat16)
        source = lax.broadcasted_iota(jnp.int32, (total, total), 0) // kinds
        target = lax.broadcasted_iota(jnp.int32, (total, total), 1) // kinds
        earlier = jnp.where(source < target, 1.0, 0.0).astype(jnp.bfloat16)
        same = jnp.where(source == target, 1.0, 0.0).astype(jnp.bfloat16)
        over = (((0,), (0,)), ((), ()))
        arrival = lax.dot_general(full, earlier, over, preferred_element_type=jnp.float32)[0:1]
        filled = lax.dot_general(full, same, over, preferred_element_type=jnp.float32)[0:1]
        arrival = jnp.where(filled > 0.5, arrival, -1.0).astype(jnp.int32)
        here = rank_ref[...] == arrival
        kind = lax.broadcasted_iota(jnp.int32, (tokens, total), 1) % kinds
        for k in range(kinds):
            placer[k] = jnp.where(here & (kind == k), 1.0, 0.0).astype(jnp.bfloat16)
        count = jnp.sum(full[:, 0:1].astype(jnp.float32)).astype(jnp.int32)
        covered[...] = jnp.where(rank_ref[...] < count, 1, 0) * jnp.ones((1, 128), jnp.int32)

    last = lax.broadcasted_iota(jnp.int32, (tokens, width), 0) == tokens - 1
    taken = jnp.concatenate([covered[...]] * (width // 128), axis=1) > 0
    for k in range(kinds):
        inserted = jnp.dot(placer[k], rows, preferred_element_type=jnp.float32)
        own = jnp.where(last, edge_ref[k : k + 1], scaled_ref[k].astype(jnp.float32))
        out_ref[k] = jnp.where(taken, inserted, own).astype(out_ref.dtype)


def place(arrived, rank, edge, scaled):
    slots, kinds, features = arrived.shape
    _, tokens, _ = scaled.shape
    width = 256
    return pl.pallas_call(
        place_kernel,
        name="place",
        grid=(features // width,),
        in_specs=[
            pl.BlockSpec((slots, kinds, width), lambda i: (0, 0, i)),
            pl.BlockSpec((tokens, 1), lambda i: (0, 0)),
            pl.BlockSpec((8, width), lambda i: (0, i)),
            pl.BlockSpec((kinds, tokens, width), lambda i: (0, 0, i)),
        ],
        out_specs=pl.BlockSpec((kinds, tokens, width), lambda i: (0, 0, i)),
        out_shape=jax.ShapeDtypeStruct(scaled.shape, scaled.dtype),
        scratch_shapes=[
            pltpu.VMEM((kinds, tokens, slots * kinds), jnp.bfloat16),
            pltpu.VMEM((tokens, 128), jnp.int32),
        ],
        cost_estimate=pl.CostEstimate(
            flops=2 * kinds * tokens * slots * kinds * features,
            bytes_accessed=2 * (slots * kinds + 2 * kinds * tokens) * features,
            transcendentals=0,
        ),
    )(arrived, rank, edge, scaled)


def passed_back(block, axis):
    devices = lax.axis_size(axis)
    return lax.ppermute(block, axis, [((i + 1) % devices, i) for i in range(devices)])


def per_device(directions, magnitudes, outlier_rows, outlier_counts, destinations, retention_order):
    slab_count = lax.axis_size(SLAB)
    tokens, features = directions.shape[1], directions.shape[2]
    heads = magnitudes.shape[1]
    head_size = features // heads
    pair_cap = max(2, tokens // slab_count)

    edge = jnp.concatenate(
        [directions[:, 0, :].astype(jnp.float32).reshape(-1), magnitudes[:, :, 0].reshape(-1)]
    )
    edge = passed_back(edge, SLAB)
    packed = pack(outlier_rows, destinations, outlier_counts, slab_count, pair_cap)
    arrived = lax.all_to_all(packed, SLAB, split_axis=0, concat_axis=0, tiled=True)

    edge_dirs = edge[: 2 * features].reshape(1, 2, heads, head_size)
    edge_mags = edge[2 * features :].reshape(2, 2, heads, 1)
    edge_row = (edge_mags * edge_dirs).astype(jnp.bfloat16).astype(jnp.float32).reshape(4, features)
    edge_row = jnp.concatenate([edge_row, edge_row], axis=0)
    factors = jnp.roll(magnitudes, -1, axis=2)[:, :, :, None]
    scaled = scale(directions, factors)
    sequence = retention_order[0]
    positions = jnp.arange(tokens, dtype=jnp.int32)
    rank = jnp.sum(
        jnp.where(sequence[None, :] == positions[:, None], positions[None, :], 0), axis=1, keepdims=True
    )
    return place(arrived, rank, edge_row, scaled)


def solution(mesh):
    finer = Mesh(
        mesh.devices.reshape(8, 4, 4, mesh.shape["head"]), ("slab_0", "slab_1", "slab_2", "head")
    )
    placed = (
        P(None, SLAB, "head"),
        P(None, "head", SLAB),
        P(SLAB, None, "head"),
        P(SLAB),
        P(SLAB, None),
        P(SLAB, None),
    )
    return jax.shard_map(
        per_device, mesh=finer, in_specs=placed, out_specs=P(None, SLAB, "head"), check_vma=False
    )
```

time: 226 us -> 156 us (0.69)
  the two profiles are of different devices: /device:TPU:30 before, /device:TPU:8 now
where the time goes in v1:
time: 156 us; the launch traced here: 155 us
  waiting for transfers between devices  98 us (63%)
  Pallas kernels  30.4 us (19%)
  starting transfers between devices  17.2 us (11%)
  local copies, waits for them, and re-layouts  6.7 us (4%)
  other arithmetic  1.83 us (1%)
    all_to_all x1, waiting for transfers between devices, per_device(): lax.all_to_all(packed, SLAB, split_axis=0, concat_axis=0, tiled=True)  98 us
    all_to_all x1, starting transfers between devices, per_device(): lax.all_to_all(packed, SLAB, split_axis=0, concat_axis=0, tiled=True)  16.1 us
    pallas_call x1, Pallas kernels, place(): pl.pallas_call(place_kernel, name='place', grid=(features // width,), in_...  14.2 us
    pallas_call x1, Pallas kernels, scale(): pl.pallas_call(scale_kernel, name='scale', grid=(features // width,), in_...  11 us
    broadcast_in_dim x1, local copies, waits for them, and re-layouts, per_device(): factors = jnp.roll(magnitudes, -1, axis=2)[:, :, :, None]  5.5 us
    pallas_call x1, Pallas kernels, pack(): pl.pallas_call(lambda *refs: pack_kernel(pair_cap, *refs), name='pack', i...  5.16 us
  transfers between devices with their start and end apart: 2, of which 1 were waited for; matrix products, arithmetic and copies ran while one was open for 6% of the time, Pallas kernels for 7%

profile of v1, /device:TPU:8, one launch (start us, length us, event | category | flops | bytes accessed | tf_op | source)
XLA Modules:
  0.0 154.8 jit_solution(16860708829448459726)
XLA Ops:
  0.7 5.2 %pack.1 = bf16[256,4,2560]{2,1,0:T(4,128)(2,1)} custom-call(s32[128]{0:T(128)} %bitcast.18, s32[1]{0:T(128)S(6)} %copy.18.refs_1_, bf16[128,4,2560]{2,1,0:T(4,128)(2,1)} %refs_2_.1), custom_call_target="tpu_custom_call" | custom-call | bytes 7864320 | tf_op jit(solution)/shard_map/pack/pallas_call | solution.py:50
  5.8 0.0 copy-start
  5.8 0.0 copy-start.1
  5.8 16.1 %all-to-all-start = ((bf16[256,4,2560]{2,1,0:T(4,128)(2,1)}), bf16[256,4,2560]{2,1,0:T(4,128)(2,1)}, u32[]{:S(2)}, u32[]{:S(2)}) async-start(bf16[256,4,2560]{2,1,0:T(4,128)(2,1)} %pack.1), calls=%async_computation | async-start | bytes 10485760 | tf_op jit(solution)/shard_map/all_to_all | solution.py:176
  22.0 0.0 copy-done
  22.0 0.1 copy.12
  22.1 0.1 reshape_squeeze.3
  22.2 0.9 slice_convert_fusion
  23.1 1.0 collective-permute-start
  24.2 0.1 slice.30
  24.3 0.0 copy-done.1
  24.3 0.1 select_reduce_fusion
  24.4 0.1 maximum_bitcast_fusion
  24.5 5.5 %copy.13.mags_ref = f32[4,20,256,1]{3,2,1,0:T(8,128)} copy(f32[4,20,256,1]{2,0,1,3:T(4,128)S(1)} %maximum_bitcast_fusion) | data formatting | bytes 163840 | tf_op jit(solution)/shard_map/broadcast_in_dim | solution.py:182
  30.0 0.8 copy.14.rank_ref
  30.8 11.0 %scale.1.scaled_ref = bf16[4,256,2560]{2,1,0:T(8,128)(2,1)} custom-call(bf16[2,256,2560]{2,1,0:T(8,128)(2,1)} %dirs_ref.1, f32[4,20,256,1]{3,2,1,0:T(8,128)} %copy.13.mags_ref), custom_call_target="tpu_custom_call" | custom-call | flops 13107200 | bytes 7864320 | tf_op jit(solution)/shard_map/scale/pallas_call | solution.py:81
  41.8 0.0 collective-permute-done
  41.8 0.1 mul.19
  41.9 0.1 multiply_convert_fusion
  42.0 0.6 maximum_convert_fusion.edge_ref
  42.7 98.0 %all-to-all-done.arrived_ref = bf16[256,4,2560]{2,1,0:T(4,128)(2,1)} async-done(((bf16[256,4,2560]{2,1,0:T(4,128)(2,1)}), bf16[256,4,2560]{2,1,0:T(4,128)(2,1)}, u32[]{:S(2)}, u32[]{:S(2)}) %all-to-all-start) | async-done | bytes 5242912 | tf_op jit(solution)/shard_map/all_to_all | solution.py:176
  140.6 14.2 %place.1 = bf16[4,256,2560]{2,1,0:T(8,128)(2,1)} custom-call(bf16[256,4,2560]{2,1,0:T(4,128)(2,1)} %all-to-all-done.arrived_ref, s32[256,1]{1,0:T(8,128)} %copy.14.rank_ref, f32[8,2560]{1,0:T(8,128)} %maximum_convert_fusion.edge_ref, bf16[4,256,2560]{2,1,0:T(8,128)(2,1)} %scale.1.scaled_ref), custom_call_target="tpu_custom_call" | custom-call | flops 5368709120 | bytes 15728640 | tf_op jit(solution)/shard_map/place/pallas_call | solution.py:135
  (6 shorter events, 0.0 us)
Async XLA Ops:
  5.8 16.2 %copy-start = (f32[4,20,256]{2,0,1:T(4,128)S(1)}, f32[4,20,256]{2,0,1:T(4,128)}, u32[]{:S(2)}) copy-start(f32[4,20,256]{2,0,1:T(4,128)} %param.7) | copy-start | bytes 245764
  5.8 18.4 %copy-start.1 = (s32[1,256]{1,0:T(1,128)S(1)}, s32[1,256]{1,0:T(1,128)}, u32[]{:S(2)}) copy-start(s32[1,256]{1,0:T(1,128)} %param.11) | copy-start | bytes 3076
  5.8 134.8 %all-to-all-start = ((bf16[256,4,2560]{2,1,0:T(4,128)(2,1)}), bf16[256,4,2560]{2,1,0:T(4,128)(2,1)}, u32[]{:S(2)}, u32[]{:S(2)}) async-start(bf16[256,4,2560]{2,1,0:T(4,128)(2,1)} %pack.1), calls=%async_computation | async-start | bytes 10485760 | tf_op jit(solution)/shard_map/all_to_all | solution.py:176
  23.1 18.7 %collective-permute-start = (f32[5200]{0:T(1024)S(1)}, f32[5200]{0:T(1024)S(1)}, u32[]{:S(2)}, u32[]{:S(2)}) collective-permute-start(f32[5200]{0:T(1024)S(1)} %pad_maximum_fusion), channel_id=1, source_target_pairs={{2,0},{4,2},{6,4},{8,6},{10,8},{12,10},{14,12},{16,14},{18,16},{20... | collective-permute-start | bytes 62408 | tf_op jit(solution)/shard_map/ppermute | solution.py:161

commit v2 on v1

v2 whole, which is shorter than its diff:
```python
import jax
import jax.numpy as jnp
from jax import lax
from jax.experimental import pallas as pl
from jax.experimental.pallas import tpu as pltpu
from jax.sharding import Mesh
from jax.sharding import PartitionSpec as P

SLAB = ("slab_0", "slab_1", "slab_2")
EMPTY = 2.0**127
WIDTH = 512
DEPTH = 2


def pack_kernel(pair_cap, dest_ref, count_ref, rows_ref, out_ref, held, blank, seen, slot, in_sem, out_sem):
    slabs = seen.shape[0]
    parts = in_sem.shape[0]
    size = held.shape[0] // parts

    def fetch(p):
        part = pl.ds(p * size, size)
        return pltpu.make_async_copy(rows_ref.at[part], held.at[part], in_sem.at[p])

    for p in range(parts):
        fetch(p).start()
    blank[...] = jnp.full(blank.shape, EMPTY, blank.dtype)

    def clear(i, carry):
        seen[i] = 0
        return carry

    lax.fori_loop(0, slabs, clear, 0, unroll=8)
    live = count_ref[0]

    def number(r, carry):
        d = dest_ref[r]
        j = seen[d]
        seen[d] = j + 1
        slot[r] = d * pair_cap + j
        return carry

    lax.fori_loop(0, live, number, 0)

    def leave(d, carry):
        for j in range(pair_cap):

            @pl.when(seen[d] <= j)
            def _():
                pltpu.make_async_copy(blank.at[0], out_ref.at[d * pair_cap + j], out_sem).start()

        return carry

    lax.fori_loop(0, slabs, leave, 0, unroll=4)
    for p in range(parts):
        fetch(p).wait()

    def send(r, carry):
        pltpu.make_async_copy(held.at[r], out_ref.at[slot[r]], out_sem).start()
        return carry

    lax.fori_loop(0, live, send, 0)
    pltpu.make_async_copy(out_ref, out_ref, out_sem).wait()


def pack(outlier_rows, destinations, outlier_counts, slab_count, pair_cap):
    row_slots, kinds, features = outlier_rows.shape
    smem = pl.BlockSpec(memory_space=pltpu.SMEM)
    anywhere = pl.BlockSpec(memory_space=pl.ANY)
    return pl.pallas_call(
        lambda *refs: pack_kernel(pair_cap, *refs),
        name="pack",
        in_specs=[smem, smem, anywhere],
        out_specs=anywhere,
        out_shape=jax.ShapeDtypeStruct((slab_count * pair_cap, kinds, features), outlier_rows.dtype),
        scratch_shapes=[
            pltpu.VMEM(outlier_rows.shape, outlier_rows.dtype),
            pltpu.VMEM((1, kinds, features), outlier_rows.dtype),
            pltpu.SMEM((slab_count,), jnp.int32),
            pltpu.SMEM((row_slots,), jnp.int32),
            pltpu.SemaphoreType.DMA((4,)),
            pltpu.SemaphoreType.DMA,
        ],
        cost_estimate=pl.CostEstimate(
            flops=0, bytes_accessed=3 * row_slots * kinds * features * 2, transcendentals=0
        ),
    )(destinations[:, 0], outlier_counts, outlier_rows)


def shift_kernel(dirs_ref, edge_ref, out_ref):
    tokens, width = dirs_ref.shape[1], dirs_ref.shape[2]
    last = lax.broadcasted_iota(jnp.int32, (tokens, width), 0) == tokens - 1
    for v in range(2):
        ahead = pltpu.roll(dirs_ref[v].astype(jnp.float32), tokens - 1, 0)
        out_ref[v] = jnp.where(last, edge_ref[v : v + 1], ahead).astype(out_ref.dtype)


def shift(directions, edge):
    _, tokens, features = directions.shape
    width = 256
    return pl.pallas_call(
        shift_kernel,
        name="shift",
        compiler_params=pltpu.CompilerParams(vmem_limit_bytes=16 * 2**20),
        grid=(features // width,),
        in_specs=[
            pl.BlockSpec((2, tokens, width), lambda i: (0, 0, i)),
            pl.BlockSpec((2, width), lambda i: (0, i)),
        ],
        out_specs=pl.BlockSpec((2, tokens, width), lambda i: (0, 0, i)),
        out_shape=jax.ShapeDtypeStruct(directions.shape, directions.dtype),
        cost_estimate=pl.CostEstimate(
            flops=20 * tokens * features, bytes_accessed=8 * tokens * features, transcendentals=0
        ),
    )(directions, edge)


def place_kernel(arrived, rank, dirs, mags, out, a_buf, r_buf, d_buf, m_buf, o_buf, placer, covered, wide, a_sem, r_sem, d_sem, m_sem, o_sem):
    blocks, slots, kinds, width = a_buf.shape
    tokens = o_buf.shape[2]
    lanes = 128
    chunks = slots // lanes
    heads = width // lanes

    def columns(i):
        return pl.ds(pl.multiple_of(i * width, lanes), width)

    def a_copy(i):
        return pltpu.make_async_copy(arrived.at[:, :, columns(i)], a_buf.at[i], a_sem.at[i])

    def d_copy(i):
        return pltpu.make_async_copy(dirs.at[:, :, columns(i)], d_buf.at[i], d_sem.at[i])

    def o_copy(i):
        return pltpu.make_async_copy(o_buf.at[i], out.at[:, :, columns(i)], o_sem.at[i])

    r_copy = pltpu.make_async_copy(rank, r_buf, r_sem)
    m_copy = pltpu.make_async_copy(mags, m_buf, m_sem)
    a_copy(0).start()
    r_copy.start()
    m_copy.start()
    d_copy(0).start()
    for i in range(1, DEPTH):
        a_copy(i).start()
        d_copy(i).start()

    r_copy.wait()
    m_copy.wait()

    def block(i, carry):
        @pl.when(i + DEPTH < blocks)
        def _():
            a_copy(i + DEPTH).start()
            d_copy(i + DEPTH).start()

        a_copy(i).wait()
        for c in range(heads):
            wide[c] = (
                a_buf[i, :, :, c * lanes : (c + 1) * lanes]
                .reshape(slots * kinds, lanes)
                .astype(jnp.float32)
            )

        @pl.when(i == 0)
        def _():
            first = wide[0, pl.ds(0, slots, stride=kinds), :]
            full = jnp.where(first < EMPTY, 1.0, 0.0).astype(jnp.bfloat16)
            corner = jnp.where(lax.broadcasted_iota(jnp.int32, (8, lanes), 1) == 0, 1.0, 0.0)
            corner = corner.astype(jnp.bfloat16)
            chunk = lax.broadcasted_iota(jnp.int32, (chunks, lanes), 0)
            over = (((1,), (1,)), ((), ()))
            filled = jnp.zeros((chunks, lanes), jnp.float32)
            for c in range(chunks):
                flags = lax.dot_general(
                    corner, full[c * lanes : (c + 1) * lanes], over, preferred_element_type=jnp.float32
                )
                filled = jnp.where(chunk == c, flags[0:1], filled)
            ones = filled.astype(jnp.bfloat16)
            source = lax.broadcasted_iota(jnp.int32, (lanes, lanes), 0)
            target = lax.broadcasted_iota(jnp.int32, (lanes, lanes), 1)
            tri = jnp.where(source < target, 1.0, 0.0).astype(jnp.bfloat16)
            inside = jnp.dot(ones, tri, preferred_element_type=jnp.float32)
            sums = jnp.dot(ones, jnp.ones((lanes, lanes), jnp.bfloat16), preferred_element_type=jnp.float32)
            ahead = jnp.zeros_like(sums)
            run = jnp.zeros((1, lanes), jnp.float32)
            for c in range(chunks):
                ahead = jnp.where(chunk == c, run, ahead)
                run = run + sums[c : c + 1]
            arrival = jnp.where(filled > 0.5, inside + ahead, -1.0).astype(jnp.int32)
            place_of = r_buf[...]
            covered[...] = jnp.where(place_of < run.astype(jnp.int32), 1, 0)
            for c in range(chunks):
                placer[:, c * lanes : (c + 1) * lanes] = jnp.where(
                    place_of == arrival[c : c + 1], 1.0, 0.0
                ).astype(jnp.bfloat16)

        d_copy(i).wait()
        factors = m_buf[i]
        own_dirs = [d_buf[i, v].astype(jnp.float32) for v in range(2)]
        taken = covered[...] > 0
        for k in range(kinds):
            rows = jnp.concatenate(
                [wide[c, pl.ds(k, slots, stride=kinds), :] for c in range(heads)], axis=1
            ).astype(jnp.bfloat16)
            inserted = jnp.dot(placer[...], rows, preferred_element_type=jnp.float32)
            for c in range(heads):
                part = slice(c * lanes, (c + 1) * lanes)
                own = factors[:, k * heads + c : k * heads + c + 1] * own_dirs[k % 2][:, part]
                o_buf[i, k, :, part] = jnp.where(taken, inserted[:, part], own).astype(o_buf.dtype)
        o_copy(i).start()
        return carry

    lax.fori_loop(0, blocks, block, 0)
    for i in range(blocks):
        o_copy(i).wait()


def place(arrived, rank, dirs, mags):
    slots, kinds, features = arrived.shape
    _, tokens, _ = dirs.shape
    width = WIDTH
    blocks = features // width
    anywhere = pl.BlockSpec(memory_space=pl.ANY)
    return pl.pallas_call(
        place_kernel,
        name="place",
        in_specs=[anywhere] * 4,
        out_specs=anywhere,
        out_shape=jax.ShapeDtypeStruct((kinds, tokens, features), arrived.dtype),
        scratch_shapes=[
            pltpu.VMEM((blocks, slots, kinds, width), arrived.dtype),
            pltpu.VMEM(rank.shape, rank.dtype),
            pltpu.VMEM((blocks, 2, tokens, width), dirs.dtype),
            pltpu.VMEM(mags.shape, mags.dtype),
            pltpu.VMEM((blocks, kinds, tokens, width), arrived.dtype),
            pltpu.VMEM((tokens, slots), jnp.bfloat16),
            pltpu.VMEM((tokens, 128), jnp.int32),
            pltpu.VMEM((width // 128, slots * kinds, 128), jnp.float32),
            pltpu.SemaphoreType.DMA((blocks,)),
            pltpu.SemaphoreType.DMA,
            pltpu.SemaphoreType.DMA((blocks,)),
            pltpu.SemaphoreType.DMA,
            pltpu.SemaphoreType.DMA((blocks,)),
        ],
        cost_estimate=pl.CostEstimate(
            flops=2 * kinds * tokens * slots * features,
            bytes_accessed=2 * (slots * kinds + 2 * tokens + kinds * tokens) * features,
            transcendentals=0,
        ),
    )(arrived, rank, dirs, mags)


def passed_back(block, axis):
    devices = lax.axis_size(axis)
    return lax.ppermute(block, axis, [((i + 1) % devices, i) for i in range(devices)])


def per_device(directions, magnitudes, outlier_rows, outlier_counts, destinations, retention_order):
    slab_count = lax.axis_size(SLAB)
    tokens, features = directions.shape[1], directions.shape[2]
    heads = magnitudes.shape[1]
    head_size = features // heads
    pair_cap = max(2, tokens // slab_count)

    edge = jnp.concatenate(
        [directions[:, 0, :].astype(jnp.float32).reshape(-1), magnitudes[:, :, 0].reshape(-1)]
    )
    edge = passed_back(edge, SLAB)
    packed = pack(outlier_rows, destinations, outlier_counts, slab_count, pair_cap)
    packed, edge = lax.optimization_barrier((packed, edge))
    arrived = lax.all_to_all(packed, SLAB, split_axis=0, concat_axis=0, tiled=True)

    edge_dirs = edge[: 2 * features].reshape(2, features)
    edge_mags = edge[2 * features :].reshape(4, heads, 1)
    factors = jnp.concatenate([magnitudes[:, :, 1:], edge_mags], axis=2)
    blocks = features // WIDTH
    factors = factors.reshape(4, blocks, heads // blocks, tokens).transpose(1, 3, 0, 2)
    factors = factors.reshape(blocks, tokens, 4 * heads // blocks)
    factors = jnp.pad(factors, ((0, 0), (0, 0), (0, 128 - factors.shape[2])))
    sequence = retention_order[0]
    positions = jnp.arange(tokens, dtype=jnp.int32)
    rank = jnp.sum(
        jnp.where(sequence[None, :] == positions[:, None], positions[None, :], 0), axis=1, keepdims=True
    )
    rank = jnp.broadcast_to(rank, (tokens, 128))
    factors, edge_dirs, rank = lax.optimization_barrier((factors, edge_dirs, rank))
    return place(arrived, rank, shift(directions, edge_dirs), factors)


def solution(mesh):
    finer = Mesh(
        mesh.devices.reshape(8, 4, 4, mesh.shape["head"]), ("slab_0", "slab_1", "slab_2", "head")
    )
    placed = (
        P(None, SLAB, "head"),
        P(None, "head", SLAB),
        P(SLAB, None, "head"),
        P(SLAB),
        P(SLAB, None),
        P(SLAB, None),
    )
    return jax.shard_map(
        per_device, mesh=finer, in_specs=placed, out_specs=P(None, SLAB, "head"), check_vma=False
    )
```

time: 156 us -> 151 us (0.968)
  Pallas kernels: 30.4 us -> 13 us
  waiting for transfers between devices: 98 us -> 112 us
  starting transfers between devices: 17.2 us -> 19.1 us
  local copies, waits for them, and re-layouts: 6.7 us -> 4.91 us
    pallas_call x2, Pallas kernels: 25.2 us -> 9.34 us  [the longest x1 8.25 us: place(): pl.pallas_call(place_kernel, name='place', in_specs=[anywhere] * 4, out_s...]
    all_to_all x1, waiting for transfers between devices: 98 us -> 112 us  [per_device(): lax.all_to_all(packed, SLAB, split_axis=0, concat_axis=0, tiled=True)]
    broadcast_in_dim x2 -> x1, local copies, waits for them, and re-layouts: 6.29 us -> 0.75 us  [per_device(): rank = jnp.broadcast_to(rank, (tokens, 128))]
  transfers between devices with their start and end apart: 2 -> 2, of which waited for: 1 -> 1; matrix products, arithmetic and copies ran while one was open for 6% -> 2% of each run, Pallas kernels for 7% -> 3%
where the time goes in v2:
time: 151 us
  waiting for transfers between devices  112 us (74%)
  starting transfers between devices  19.1 us (13%)
  Pallas kernels  13 us (9%)
  local copies, waits for them, and re-layouts  4.91 us (3%)
    all_to_all x1, waiting for transfers between devices, per_device(): lax.all_to_all(packed, SLAB, split_axis=0, concat_axis=0, tiled=True)  112 us
    all_to_all x1, starting transfers between devices, per_device(): lax.all_to_all(packed, SLAB, split_axis=0, concat_axis=0, tiled=True)  16.9 us
    pallas_call x1, Pallas kernels, place(): pl.pallas_call(place_kernel, name='place', in_specs=[anywhere] * 4, out_s...  8.25 us
    pallas_call x1, Pallas kernels, pack(): pl.pallas_call(lambda *refs: pack_kernel(pair_cap, *refs), name='pack', i...  3.62 us
  transfers between devices with their start and end apart: 2, of which 1 were waited for; matrix products, arithmetic and copies ran while one was open for 2% of the time, Pallas kernels for 3%

profile of v2, /device:TPU:8, one launch (start us, length us, event | category | flops | bytes accessed | tf_op | source)
XLA Modules:
  0.0 150.8 jit_solution(10656660494904641502)
XLA Ops:
  0.0 0.9 slice_convert_fusion
  0.9 0.8 slice.24
  1.7 0.1 copy.14
  1.8 0.1 reshape_squeeze.3
  1.9 2.2 %collective-permute-start = (f32[5200]{0:T(1024)S(1)}, f32[5200]{0:T(1024)S(1)}, u32[]{:S(2)}, u32[]{:S(2)}) collective-permute-start(f32[5200]{0:T(1024)S(1)} %pad_maximum_fusion), channel_id=1, source_target_pairs={{2,0},{4,2},{6,4},{8,6},{10,8},{12,10},{14,12},{16,14},{18,16},{20... | collective-permute-start | bytes 62408 | tf_op jit(solution)/shard_map/ppermute | solution.py:254
  4.7 3.6 %pack.1 = bf16[256,4,2560]{2,1,0:T(4,128)(2,1)} custom-call(s32[128]{0:T(128)} %bitcast.13, s32[1]{0:T(128)S(6)} %copy.18.refs_1_, bf16[128,4,2560]{2,1,0:T(4,128)(2,1)} %refs_2_.1), custom_call_target="tpu_custom_call" | custom-call | bytes 7864320 | tf_op jit(solution)/shard_map/pack/pallas_call | solution.py:69
  8.4 0.0 copy-start.2
  8.4 0.0 copy-start.3
  8.4 0.0 collective-permute-done
  8.4 16.9 %all-to-all-start = ((bf16[256,4,2560]{2,1,0:T(4,128)(2,1)}), bf16[256,4,2560]{2,1,0:T(4,128)(2,1)}, u32[]{:S(2)}, u32[]{:S(2)}) async-start(bf16[256,4,2560]{2,1,0:T(4,128)(2,1)} %pack.1), calls=%async_computation | async-start | bytes 10485760 | tf_op jit(solution)/shard_map/all_to_all | solution.py:270
  25.3 0.0 copy-done.2
  25.3 0.0 copy-start.1
  25.3 0.1 slice.25
  25.4 0.0 copy-done.3
  25.4 0.1 select_reduce_fusion
  25.6 0.1 concatenate.13
  25.7 0.2 copy.16
  25.9 0.1 maximum_bitcast_fusion
  26.1 0.2 copy.17
  26.3 0.9 pad.4.mags
  27.3 0.8 broadcast_in_dim.22.rank
  28.0 0.0 copy-done.1
  28.0 1.1 shift.1.dirs
  29.1 0.0 copy-start
  29.1 1.5 copy-done
  30.6 112.0 %all-to-all-done.arrived = bf16[256,4,2560]{2,1,0:T(4,128)(2,1)} async-done(((bf16[256,4,2560]{2,1,0:T(4,128)(2,1)}), bf16[256,4,2560]{2,1,0:T(4,128)(2,1)}, u32[]{:S(2)}, u32[]{:S(2)}) %all-to-all-start) | async-done | bytes 5242912 | tf_op jit(solution)/shard_map/all_to_all | solution.py:270
  142.6 8.2 %place.1 = bf16[4,256,2560]{2,1,0:T(8,128)(2,1)} custom-call(bf16[256,4,2560]{2,1,0:T(4,128)(2,1)} %all-to-all-done.arrived, s32[256,128]{1,0:T(8,128)} %broadcast_in_dim.22.rank, bf16[2,256,2560]{2,1,0:T(8,128)(2,1)} %copy-done, f32[5,256,128]{2,1,0:T(8,128)} %pad.4.mags), custom_call_target="tpu_custom_call" | custom-call | flops 1342177280 | bytes 13107200 | tf_op jit(solution)/shard_map/place/pallas_call | solution.py:223
  (6 shorter events, 0.1 us)
Async XLA Ops:
  1.9 6.5 %collective-permute-start = (f32[5200]{0:T(1024)S(1)}, f32[5200]{0:T(1024)S(1)}, u32[]{:S(2)}, u32[]{:S(2)}) collective-permute-start(f32[5200]{0:T(1024)S(1)} %pad_maximum_fusion), channel_id=1, source_target_pairs={{2,0},{4,2},{6,4},{8,6},{10,8},{12,10},{14,12},{16,14},{18,16},{20... | collective-permute-start | bytes 62408 | tf_op jit(solution)/shard_map/ppermute | solution.py:254
  8.4 16.9 %copy-start.2 = (f32[4,20,256]{2,0,1:T(4,128)S(1)}, f32[4,20,256]{2,0,1:T(4,128)}, u32[]{:S(2)}) copy-start(f32[4,20,256]{2,0,1:T(4,128)} %param.7) | copy-start | bytes 245764
  8.4 17.1 %copy-start.3 = (s32[1,256]{1,0:T(1,128)S(1)}, s32[1,256]{1,0:T(1,128)}, u32[]{:S(2)}) copy-start(s32[1,256]{1,0:T(1,128)} %param.11) | copy-start | bytes 3076
  8.4 134.2 %all-to-all-start = ((bf16[256,4,2560]{2,1,0:T(4,128)(2,1)}), bf16[256,4,2560]{2,1,0:T(4,128)(2,1)}, u32[]{:S(2)}, u32[]{:S(2)}) async-start(bf16[256,4,2560]{2,1,0:T(4,128)(2,1)} %pack.1), calls=%async_computation | async-start | bytes 10485760 | tf_op jit(solution)/shard_map/all_to_all | solution.py:270
  25.3 2.7 %copy-start.1 = (bf16[2,256,2560]{2,1,0:T(8,128)(2,1)S(1)}, bf16[2,256,2560]{2,1,0:T(8,128)(2,1)}, u32[]{:S(2)}) copy-start(bf16[2,256,2560]{2,1,0:T(8,128)(2,1)} %dirs_ref.1) | copy-start | bytes 7864324
  29.1 1.5 copy-start

commit v3 on v2

--- a/solution.py
+++ b/solution.py
@@ -86,35 +86,47 @@
     )(destinations[:, 0], outlier_counts, outlier_rows)
 
 
-def shift_kernel(dirs_ref, edge_ref, out_ref):
-    tokens, width = dirs_ref.shape[1], dirs_ref.shape[2]
-    last = lax.broadcasted_iota(jnp.int32, (tokens, width), 0) == tokens - 1
+def prepare_kernel(dirs_ref, order_ref, out_ref, rank_ref):
+    tokens = dirs_ref.shape[1]
     for v in range(2):
         ahead = pltpu.roll(dirs_ref[v].astype(jnp.float32), tokens - 1, 0)
-        out_ref[v] = jnp.where(last, edge_ref[v : v + 1], ahead).astype(out_ref.dtype)
-
-
-def shift(directions, edge):
+        out_ref[v] = ahead.astype(out_ref.dtype)
+
+    @pl.when(pl.program_id(0) == 0)
+    def _():
+        token = lax.broadcasted_iota(jnp.int32, (tokens, tokens), 0)
+        number = lax.broadcasted_iota(jnp.int32, (tokens, tokens), 1)
+        here = jnp.where(order_ref[...] == token, number, 0).astype(jnp.float32)
+        rank = jnp.sum(here, axis=1, keepdims=True).astype(jnp.int32)
+        rank_ref[...] = jnp.broadcast_to(rank, rank_ref.shape)
+
+
+def prepare(directions, order):
     _, tokens, features = directions.shape
     width = 256
+    spec = pl.BlockSpec((2, tokens, width), lambda i: (0, 0, i))
     return pl.pallas_call(
-        shift_kernel,
-        name="shift",
+        prepare_kernel,
+        name="prepare",
         compiler_params=pltpu.CompilerParams(vmem_limit_bytes=16 * 2**20),
         grid=(features // width,),
-        in_specs=[
-            pl.BlockSpec((2, tokens, width), lambda i: (0, 0, i)),
-            pl.BlockSpec((2, width), lambda i: (0, i)),
+        in_specs=[spec, pl.BlockSpec((1, tokens), lambda i: (0, 0))],
+        out_specs=[spec, pl.BlockSpec((tokens, 128), lambda i: (0, 0))],
+        out_shape=[
+            jax.ShapeDtypeStruct(directions.shape, directions.dtype),
+            jax.ShapeDtypeStruct((tokens, 128), jnp.int32),
         ],
-        out_specs=pl.BlockSpec((2, tokens, width), lambda i: (0, 0, i)),
-        out_shape=jax.ShapeDtypeStruct(directions.shape, directions.dtype),
         cost_estimate=pl.CostEstimate(
             flops=20 * tokens * features, bytes_accessed=8 * tokens * features, transcendentals=0
         ),
-    )(directions, edge)
-
-
-def place_kernel(arrived, rank, dirs, mags, out, a_buf, r_buf, d_buf, m_buf, o_buf, placer, covered, wide, a_sem, r_sem, d_sem, m_sem, o_sem):
+    )(directions, order)
+
+
+def place_kernel(
+    arrived, rank, dirs, mags, edge, out,
+    a_buf, r_buf, d_buf, m_buf, e_buf, o_buf, placer, covered, wide,
+    a_sem, r_sem, d_sem, m_sem, e_sem, o_sem,
+):
     blocks, slots, kinds, width = a_buf.shape
     tokens = o_buf.shape[2]
     lanes = 128
@@ -135,9 +147,11 @@
 
     r_copy = pltpu.make_async_copy(rank, r_buf, r_sem)
     m_copy = pltpu.make_async_copy(mags, m_buf, m_sem)
+    e_copy = pltpu.make_async_copy(edge, e_buf, e_sem)
     a_copy(0).start()
     r_copy.start()
     m_copy.start()
+    e_copy.start()
     d_copy(0).start()
     for i in range(1, DEPTH):
         a_copy(i).start()
@@ -145,6 +159,7 @@
 
     r_copy.wait()
     m_copy.wait()
+    e_copy.wait()
 
     def block(i, carry):
         @pl.when(i + DEPTH < blocks)
@@ -194,6 +209,14 @@
                 ).astype(jnp.bfloat16)
 
         d_copy(i).wait()
+        tail = slice(tokens - 16, tokens)
+        last = lax.broadcasted_iota(jnp.int32, (16, width), 0) == 15
+        for v in range(2):
+            end = d_buf[i, v, tail].astype(jnp.float32)
+            end = jnp.where(last, e_buf[v : v + 1, columns(i)], end)
+            d_buf[i, v, tail] = end.astype(d_buf.dtype)
+        given = e_buf[2:3, pl.ds(pl.multiple_of(i * lanes, lanes), lanes)]
+        m_buf[i, tail] = jnp.where(last[:, 0:lanes], given, m_buf[i, tail])
         factors = m_buf[i]
         own_dirs = [d_buf[i, v].astype(jnp.float32) for v in range(2)]
         taken = covered[...] > 0
@@ -214,7 +237,7 @@
         o_copy(i).wait()
 
 
-def place(arrived, rank, dirs, mags):
+def place(arrived, rank, dirs, mags, edge):
     slots, kinds, features = arrived.shape
     _, tokens, _ = dirs.shape
     width = WIDTH
@@ -223,7 +246,7 @@
     return pl.pallas_call(
         place_kernel,
         name="place",
-        in_specs=[anywhere] * 4,
+        in_specs=[anywhere] * 5,
         out_specs=anywhere,
         out_shape=jax.ShapeDtypeStruct((kinds, tokens, features), arrived.dtype),
         scratch_shapes=[
@@ -231,6 +254,7 @@
             pltpu.VMEM(rank.shape, rank.dtype),
             pltpu.VMEM((blocks, 2, tokens, width), dirs.dtype),
             pltpu.VMEM(mags.shape, mags.dtype),
+            pltpu.VMEM(edge.shape, edge.dtype),
             pltpu.VMEM((blocks, kinds, tokens, width), arrived.dtype),
             pltpu.VMEM((tokens, slots), jnp.bfloat16),
             pltpu.VMEM((tokens, 128), jnp.int32),
@@ -239,6 +263,7 @@
             pltpu.SemaphoreType.DMA,
             pltpu.SemaphoreType.DMA((blocks,)),
             pltpu.SemaphoreType.DMA,
+            pltpu.SemaphoreType.DMA,
             pltpu.SemaphoreType.DMA((blocks,)),
         ],
         cost_estimate=pl.CostEstimate(
@@ -246,7 +271,7 @@
             bytes_accessed=2 * (slots * kinds + 2 * tokens + kinds * tokens) * features,
             transcendentals=0,
         ),
-    )(arrived, rank, dirs, mags)
+    )(arrived, rank, dirs, mags, edge)
 
 
 def passed_back(block, axis):
@@ -261,29 +286,28 @@
     head_size = features // heads
     pair_cap = max(2, tokens // slab_count)
 
+    packed = pack(outlier_rows, destinations, outlier_counts, slab_count, pair_cap)
+    arrived = lax.all_to_all(packed, SLAB, split_axis=0, concat_axis=0, tiled=True)
+
+    blocks = features // WIDTH
+
+    def by_block(block):
+        count = block.shape[2]
+        block = block.reshape(4, blocks, heads // blocks, count).transpose(1, 3, 0, 2)
+        block = block.reshape(blocks, count, 4 * heads // blocks)
+        return jnp.pad(block, ((0, 0), (0, 0), (0, 128 - block.shape[2])))
+
+    first_mags = by_block(magnitudes[:, :, :1]).reshape(1, blocks * 128)
     edge = jnp.concatenate(
-        [directions[:, 0, :].astype(jnp.float32).reshape(-1), magnitudes[:, :, 0].reshape(-1)]
+        [
+            directions[:, 0, :].astype(jnp.float32),
+            jnp.pad(first_mags, ((0, 1), (0, features - blocks * 128))),
+        ]
     )
     edge = passed_back(edge, SLAB)
-    packed = pack(outlier_rows, destinations, outlier_counts, slab_count, pair_cap)
-    packed, edge = lax.optimization_barrier((packed, edge))
-    arrived = lax.all_to_all(packed, SLAB, split_axis=0, concat_axis=0, tiled=True)
-
-    edge_dirs = edge[: 2 * features].reshape(2, features)
-    edge_mags = edge[2 * features :].reshape(4, heads, 1)
-    factors = jnp.concatenate([magnitudes[:, :, 1:], edge_mags], axis=2)
-    blocks = features // WIDTH
-    factors = factors.reshape(4, blocks, heads // blocks, tokens).transpose(1, 3, 0, 2)
-    factors = factors.reshape(blocks, tokens, 4 * heads // blocks)
-    factors = jnp.pad(factors, ((0, 0), (0, 0), (0, 128 - factors.shape[2])))
-    sequence = retention_order[0]
-    positions = jnp.arange(tokens, dtype=jnp.int32)
-    rank = jnp.sum(
-        jnp.where(sequence[None, :] == positions[:, None], positions[None, :], 0), axis=1, keepdims=True
-    )
-    rank = jnp.broadcast_to(rank, (tokens, 128))
-    factors, edge_dirs, rank = lax.optimization_barrier((factors, edge_dirs, rank))
-    return place(arrived, rank, shift(directions, edge_dirs), factors)
+    factors = by_block(jnp.roll(magnitudes, -1, axis=2))
+    dirs, rank = prepare(directions, retention_order)
+    return place(arrived, rank, dirs, factors, edge)
 
 
 def solution(mesh):

time: 151 us -> 148 us (0.980)
  starting transfers between devices: 19.1 us -> 16.7 us
    ppermute x1, waiting for transfers between devices: 0.01 us -> 1.59 us  [passed_back(): lax.ppermute(block, axis, [((i + 1) % devices, i) for i in range(devices)])]
  transfers between devices with their start and end apart: 2 -> 2, of which waited for: 1 -> 2; matrix products, arithmetic and copies ran while one was open for 2% -> 1% of each run, Pallas kernels for 3% -> 1%
where the time goes in v3:
time: 148 us
  waiting for transfers between devices  112 us (76%)
  starting transfers between devices  16.7 us (11%)
  Pallas kernels  13.8 us (9%)
  local copies, waits for them, and re-layouts  3.79 us (3%)
    all_to_all x1, waiting for transfers between devices, per_device(): lax.all_to_all(packed, SLAB, split_axis=0, concat_axis=0, tiled=True)  111 us
    all_to_all x1, starting transfers between devices, per_device(): lax.all_to_all(packed, SLAB, split_axis=0, concat_axis=0, tiled=True)  15.7 us
    pallas_call x1, Pallas kernels, place(): pl.pallas_call(place_kernel, name='place', in_specs=[anywhere] * 5, out_s...  8.5 us
    pallas_call x1, Pallas kernels, pack(): pl.pallas_call(lambda *refs: pack_kernel(pair_cap, *refs), name='pack', i...  4.04 us
  transfers between devices with their start and end apart: 2, of which 2 were waited for; matrix products, arithmetic and copies ran while one was open for 1% of the time, Pallas kernels for 1%

profile of v3, /device:TPU:8, one launch (start us, length us, event | category | flops | bytes accessed | tf_op | source)
XLA Modules:
  0.0 147.5 jit_solution(15297495782485679826)
XLA Ops:
  0.7 4.0 %pack.1 = bf16[256,4,2560]{2,1,0:T(4,128)(2,1)} custom-call(s32[128]{0:T(128)} %bitcast.20, s32[1]{0:T(128)S(6)} %copy.22.refs_1_, bf16[128,4,2560]{2,1,0:T(4,128)(2,1)} %refs_2_.1), custom_call_target="tpu_custom_call" | custom-call | bytes 7864320 | tf_op jit(solution)/shard_map/pack/pallas_call | solution.py:69
  4.7 0.0 copy-start.4
  4.7 0.0 copy-start
  4.7 0.0 copy-start.3
  4.7 15.7 %all-to-all-start = ((bf16[256,4,2560]{2,1,0:T(4,128)(2,1)}), bf16[256,4,2560]{2,1,0:T(4,128)(2,1)}, u32[]{:S(2)}, u32[]{:S(2)}) async-start(bf16[256,4,2560]{2,1,0:T(4,128)(2,1)} %pack.1), calls=%async_computation | async-start | bytes 10485760 | tf_op jit(solution)/shard_map/all_to_all | solution.py:290
  20.4 0.0 copy-done.4
  20.4 0.1 copy.14
  20.5 0.1 reshape.19
  20.6 0.1 reshape.20
  20.7 0.0 copy-done
  20.8 1.0 collective-permute-start
  21.8 0.1 slice.12
  21.9 0.1 pad_maximum_fusion
  22.1 0.2 copy.12
  22.3 1.0 pad.12.mags
  23.3 0.0 copy-done.3
  23.3 1.2 prepare.1
  24.6 0.0 copy-start.1
  24.6 1.5 copy-done.1
  26.0 0.0 copy-start.2
  26.0 0.7 copy-done.2
  26.7 1.6 %collective-permute-done.edge = f32[4,2560]{1,0:T(4,128)S(1)} collective-permute-done((f32[4,2560]{1,0:T(4,128)S(1)}, f32[4,2560]{1,0:T(4,128)S(1)}, u32[]{:S(2)}, u32[]{:S(2)}) %collective-permute-start) | collective-permute-done | bytes 40992 | tf_op jit(solution)/shard_map/ppermute | solution.py:279
  28.3 0.0 copy-start.5
  28.3 110.8 %all-to-all-done.arrived = bf16[256,4,2560]{2,1,0:T(4,128)(2,1)} async-done(((bf16[256,4,2560]{2,1,0:T(4,128)(2,1)}), bf16[256,4,2560]{2,1,0:T(4,128)(2,1)}, u32[]{:S(2)}, u32[]{:S(2)}) %all-to-all-start) | async-done | bytes 5242912 | tf_op jit(solution)/shard_map/all_to_all | solution.py:290
  139.0 0.0 copy-done.5
  139.0 8.5 %place.1 = bf16[4,256,2560]{2,1,0:T(8,128)(2,1)} custom-call(bf16[256,4,2560]{2,1,0:T(4,128)(2,1)} %all-to-all-done.arrived, s32[256,128]{1,0:T(8,128)} %copy-done.2, bf16[2,256,2560]{2,1,0:T(8,128)(2,1)} %copy-done.1, f32[5,256,128]{2,1,0:T(8,128)} %pad.12.mags, f32[4,2560]{1,0:T(4,128)} %copy-done.5), custom_call_target="tpu_custom_call" | custom-call | flops 1342177280 | bytes 13107200 | tf_op jit(solution)/shard_map/place/pallas_call | solution.py:246
  (8 shorter events, 0.1 us)
Async XLA Ops:
  4.7 15.7 %copy-start.4 = (f32[4,20,256]{2,0,1:T(4,128)S(1)}, f32[4,20,256]{2,0,1:T(4,128)}, u32[]{:S(2)}) copy-start(f32[4,20,256]{2,0,1:T(4,128)} %param.7) | copy-start | bytes 245764
  4.7 16.0 %copy-start = (bf16[2,256,2560]{2,1,0:T(8,128)(2,1)S(1)}, bf16[2,256,2560]{2,1,0:T(8,128)(2,1)}, u32[]{:S(2)}) copy-start(bf16[2,256,2560]{2,1,0:T(8,128)(2,1)} %dirs_ref.1) | copy-start | bytes 7864324
  4.7 18.6 %copy-start.3 = (s32[1,256]{1,0:T(1,128)S(1)}, s32[1,256]{1,0:T(1,128)}, u32[]{:S(2)}) copy-start(s32[1,256]{1,0:T(1,128)} %order_ref.1) | copy-start | bytes 3076
  4.7 134.3 %all-to-all-start = ((bf16[256,4,2560]{2,1,0:T(4,128)(2,1)}), bf16[256,4,2560]{2,1,0:T(4,128)(2,1)}, u32[]{:S(2)}, u32[]{:S(2)}) async-start(bf16[256,4,2560]{2,1,0:T(4,128)(2,1)} %pack.1), calls=%async_computation | async-start | bytes 10485760 | tf_op jit(solution)/shard_map/all_to_all | solution.py:290
  20.8 7.5 %collective-permute-start = (f32[4,2560]{1,0:T(4,128)S(1)}, f32[4,2560]{1,0:T(4,128)S(1)}, u32[]{:S(2)}, u32[]{:S(2)}) collective-permute-start(f32[4,2560]{1,0:T(4,128)S(1)} %select_maximum_fusion), channel_id=1, source_target_pairs={{2,0},{4,2},{6,4},{8,6},{10,8},{12,10},{14,12},{16,14},{18,16},{20... | collective-permute-start | bytes 122888 | tf_op jit(solution)/shard_map/ppermute | solution.py:279
  24.6 1.5 %copy-start.1 = (bf16[2,256,2560]{2,1,0:T(8,128)(2,1)}, bf16[2,256,2560]{2,1,0:T(8,128)(2,1)S(1)}, u32[]{:S(2)}) copy-start(bf16[2,256,2560]{2,1,0:T(8,128)(2,1)S(1)} %get-tuple-element.8.dirs) | copy-start | bytes 7864324
  26.0 0.7 copy-start.2
  28.3 110.8 %copy-start.5 = (f32[4,2560]{1,0:T(4,128)}, f32[4,2560]{1,0:T(4,128)S(1)}, u32[]{:S(2)}) copy-start(f32[4,2560]{1,0:T(4,128)S(1)} %collective-permute-done.edge) | copy-start | bytes 122884

commit v4 on v3

--- a/solution.py
+++ b/solution.py
@@ -15,6 +15,7 @@
 def pack_kernel(pair_cap, dest_ref, count_ref, rows_ref, out_ref, held, blank, seen, slot, in_sem, out_sem):
     slabs = seen.shape[0]
     parts = in_sem.shape[0]
+    kinds = held.shape[1]
     size = held.shape[0] // parts
 
     def fetch(p):
@@ -36,7 +37,7 @@
         d = dest_ref[r]
         j = seen[d]
         seen[d] = j + 1
-        slot[r] = d * pair_cap + j
+        slot[r] = j
         return carry
 
     lax.fori_loop(0, live, number, 0)
@@ -46,7 +47,9 @@
 
             @pl.when(seen[d] <= j)
             def _():
-                pltpu.make_async_copy(blank.at[0], out_ref.at[d * pair_cap + j], out_sem).start()
+                pltpu.make_async_copy(
+                    blank.at[0], out_ref.at[d, pl.ds(j * kinds, kinds)], out_sem
+                ).start()
 
         return carry
 
@@ -55,7 +58,9 @@
         fetch(p).wait()
 
     def send(r, carry):
-        pltpu.make_async_copy(held.at[r], out_ref.at[slot[r]], out_sem).start()
+        d = dest_ref[r]
+        first = pl.multiple_of(slot[r] * kinds, kinds)
+        pltpu.make_async_copy(held.at[r], out_ref.at[d, pl.ds(first, kinds)], out_sem).start()
         return carry
 
     lax.fori_loop(0, live, send, 0)
@@ -71,7 +76,7 @@
         name="pack",
         in_specs=[smem, smem, anywhere],
         out_specs=anywhere,
-        out_shape=jax.ShapeDtypeStruct((slab_count * pair_cap, kinds, features), outlier_rows.dtype),
+        out_shape=jax.ShapeDtypeStruct((slab_count, pair_cap * kinds, features), outlier_rows.dtype),
         scratch_shapes=[
             pltpu.VMEM(outlier_rows.shape, outlier_rows.dtype),
             pltpu.VMEM((1, kinds, features), outlier_rows.dtype),
@@ -127,8 +132,8 @@
     a_buf, r_buf, d_buf, m_buf, e_buf, o_buf, placer, covered, wide,
     a_sem, r_sem, d_sem, m_sem, e_sem, o_sem,
 ):
-    blocks, slots, kinds, width = a_buf.shape
-    tokens = o_buf.shape[2]
+    blocks, kinds, tokens, width = o_buf.shape
+    slots = a_buf.shape[1] * a_buf.shape[2] // kinds
     lanes = 128
     chunks = slots // lanes
     heads = width // lanes
@@ -157,9 +162,6 @@
         a_copy(i).start()
         d_copy(i).start()
 
-    r_copy.wait()
-    m_copy.wait()
-    e_copy.wait()
 
     def block(i, carry):
         @pl.when(i + DEPTH < blocks)
@@ -201,6 +203,9 @@
                 ahead = jnp.where(chunk == c, run, ahead)
                 run = run + sums[c : c + 1]
             arrival = jnp.where(filled > 0.5, inside + ahead, -1.0).astype(jnp.int32)
+            r_copy.wait()
+            m_copy.wait()
+            e_copy.wait()
             place_of = r_buf[...]
             covered[...] = jnp.where(place_of < run.astype(jnp.int32), 1, 0)
             for c in range(chunks):
@@ -217,18 +222,19 @@
             d_buf[i, v, tail] = end.astype(d_buf.dtype)
         given = e_buf[2:3, pl.ds(pl.multiple_of(i * lanes, lanes), lanes)]
         m_buf[i, tail] = jnp.where(last[:, 0:lanes], given, m_buf[i, tail])
-        factors = m_buf[i]
+        factors = jnp.where(covered[...] > 0, 0.0, m_buf[i])
         own_dirs = [d_buf[i, v].astype(jnp.float32) for v in range(2)]
-        taken = covered[...] > 0
         for k in range(kinds):
+          for c0 in range(0, heads, 2):
             rows = jnp.concatenate(
-                [wide[c, pl.ds(k, slots, stride=kinds), :] for c in range(heads)], axis=1
+                [wide[c, pl.ds(k, slots, stride=kinds), :] for c in range(c0, c0 + 2)], axis=1
             ).astype(jnp.bfloat16)
-            inserted = jnp.dot(placer[...], rows, preferred_element_type=jnp.float32)
-            for c in range(heads):
+            both = jnp.dot(placer[...], rows, preferred_element_type=jnp.float32)
+            for c in range(c0, c0 + 2):
                 part = slice(c * lanes, (c + 1) * lanes)
+                got = both[:, (c - c0) * lanes : (c - c0 + 1) * lanes]
                 own = factors[:, k * heads + c : k * heads + c + 1] * own_dirs[k % 2][:, part]
-                o_buf[i, k, :, part] = jnp.where(taken, inserted[:, part], own).astype(o_buf.dtype)
+                o_buf[i, k, :, part] = (got + own).astype(o_buf.dtype)
         o_copy(i).start()
         return carry
 
@@ -238,7 +244,9 @@
 
 
 def place(arrived, rank, dirs, mags, edge):
-    slots, kinds, features = arrived.shape
+    slabs, group, features = arrived.shape
+    kinds = 4
+    slots = slabs * group // kinds
     _, tokens, _ = dirs.shape
     width = WIDTH
     blocks = features // width
@@ -250,7 +258,7 @@
         out_specs=anywhere,
         out_shape=jax.ShapeDtypeStruct((kinds, tokens, features), arrived.dtype),
         scratch_shapes=[
-            pltpu.VMEM((blocks, slots, kinds, width), arrived.dtype),
+            pltpu.VMEM((blocks, slabs, group, width), arrived.dtype),
             pltpu.VMEM(rank.shape, rank.dtype),
             pltpu.VMEM((blocks, 2, tokens, width), dirs.dtype),
             pltpu.VMEM(mags.shape, mags.dtype),

time: 148 us -> 147 us (level)
  no operation moved by 1% of the time
where the time goes in v4:
time: 147 us; the launch traced here: 146 us
  waiting for transfers between devices  112 us (76%)
  starting transfers between devices  16.6 us (11%)
  Pallas kernels  12.6 us (9%)
  local copies, waits for them, and re-layouts  3.79 us (3%)
    all_to_all x1, waiting for transfers between devices, per_device(): lax.all_to_all(packed, SLAB, split_axis=0, concat_axis=0, tiled=True)  111 us
    all_to_all x1, starting transfers between devices, per_device(): lax.all_to_all(packed, SLAB, split_axis=0, concat_axis=0, tiled=True)  15.6 us
    pallas_call x1, Pallas kernels, place(): pl.pallas_call(place_kernel, name='place', in_specs=[anywhere] * 5, out_s...  7.38 us
    pallas_call x1, Pallas kernels, pack(): pl.pallas_call(lambda *refs: pack_kernel(pair_cap, *refs), name='pack', i...  4.01 us
  transfers between devices with their start and end apart: 2, of which 2 were waited for; matrix products, arithmetic and copies ran while one was open for 1% of the time, Pallas kernels for 1%

profile of v4, /device:TPU:8, one launch (start us, length us, event | category | flops | bytes accessed | tf_op | source)
XLA Modules:
  0.0 146.3 jit_solution(16524282670669218007)
XLA Ops:
  0.7 4.0 %pack.1 = bf16[128,8,2560]{2,1,0:T(8,128)(2,1)} custom-call(s32[128]{0:T(128)} %bitcast.20, s32[1]{0:T(128)S(6)} %copy.22.refs_1_, bf16[128,4,2560]{2,1,0:T(4,128)(2,1)} %refs_2_.1), custom_call_target="tpu_custom_call" | custom-call | bytes 7864320 | tf_op jit(solution)/shard_map/pack/pallas_call | solution.py:74
  4.7 0.0 copy-start.4
  4.7 0.0 copy-start
  4.7 0.0 copy-start.3
  4.7 15.6 %all-to-all-start = ((bf16[128,8,2560]{2,1,0:T(8,128)(2,1)}), bf16[128,8,2560]{2,1,0:T(8,128)(2,1)}, u32[]{:S(2)}, u32[]{:S(2)}) async-start(bf16[128,8,2560]{2,1,0:T(8,128)(2,1)} %pack.1), calls=%async_computation | async-start | bytes 10485760 | tf_op jit(solution)/shard_map/all_to_all | solution.py:298
  20.3 0.0 copy-done.4
  20.3 0.1 copy.14
  20.4 0.1 reshape.19
  20.5 0.1 reshape.20
  20.6 0.0 copy-done
  20.7 1.0 collective-permute-start
  21.7 0.1 slice.12
  21.8 0.1 pad_maximum_fusion
  22.0 0.2 copy.12
  22.2 1.0 pad.12.mags
  23.2 0.0 copy-done.3
  23.2 1.2 prepare.1
  24.5 0.0 copy-start.1
  24.5 1.5 %copy-done.1 = bf16[2,256,2560]{2,1,0:T(8,128)(2,1)} copy-done((bf16[2,256,2560]{2,1,0:T(8,128)(2,1)}, bf16[2,256,2560]{2,1,0:T(8,128)(2,1)S(1)}, u32[]{:S(2)}) %copy-start.1) | copy-done | bytes 2621464
  25.9 0.0 copy-start.2
  25.9 0.7 copy-done.2
  26.6 1.6 %collective-permute-done.edge = f32[4,2560]{1,0:T(4,128)S(1)} collective-permute-done((f32[4,2560]{1,0:T(4,128)S(1)}, f32[4,2560]{1,0:T(4,128)S(1)}, u32[]{:S(2)}, u32[]{:S(2)}) %collective-permute-start) | collective-permute-done | bytes 40992 | tf_op jit(solution)/shard_map/ppermute | solution.py:287
  28.2 0.0 copy-start.5
  28.2 110.8 %all-to-all-done.arrived = bf16[128,8,2560]{2,1,0:T(8,128)(2,1)} async-done(((bf16[128,8,2560]{2,1,0:T(8,128)(2,1)}), bf16[128,8,2560]{2,1,0:T(8,128)(2,1)}, u32[]{:S(2)}, u32[]{:S(2)}) %all-to-all-start) | async-done | bytes 5242912 | tf_op jit(solution)/shard_map/all_to_all | solution.py:298
  138.9 0.0 copy-done.5
  138.9 7.4 %place.1 = bf16[4,256,2560]{2,1,0:T(8,128)(2,1)} custom-call(bf16[128,8,2560]{2,1,0:T(8,128)(2,1)} %all-to-all-done.arrived, s32[256,128]{1,0:T(8,128)} %copy-done.2, bf16[2,256,2560]{2,1,0:T(8,128)(2,1)} %copy-done.1, f32[5,256,128]{2,1,0:T(8,128)} %pad.12.mags, f32[4,2560]{1,0:T(4,128)} %copy-done.5), custom_call_target="tpu_custom_call" | custom-call | flops 1342177280 | bytes 13107200 | tf_op jit(solution)/shard_map/place/pallas_call | solution.py:254
  (8 shorter events, 0.1 us)
Async XLA Ops:
  4.7 15.6 %copy-start.4 = (f32[4,20,256]{2,0,1:T(4,128)S(1)}, f32[4,20,256]{2,0,1:T(4,128)}, u32[]{:S(2)}) copy-start(f32[4,20,256]{2,0,1:T(4,128)} %param.7) | copy-start | bytes 245764
  4.7 15.9 %copy-start = (bf16[2,256,2560]{2,1,0:T(8,128)(2,1)S(1)}, bf16[2,256,2560]{2,1,0:T(8,128)(2,1)}, u32[]{:S(2)}) copy-start(bf16[2,256,2560]{2,1,0:T(8,128)(2,1)} %dirs_ref.1) | copy-start | bytes 7864324
  4.7 18.5 %copy-start.3 = (s32[1,256]{1,0:T(1,128)S(1)}, s32[1,256]{1,0:T(1,128)}, u32[]{:S(2)}) copy-start(s32[1,256]{1,0:T(1,128)} %order_ref.1) | copy-start | bytes 3076
  4.7 134.2 %all-to-all-start = ((bf16[128,8,2560]{2,1,0:T(8,128)(2,1)}), bf16[128,8,2560]{2,1,0:T(8,128)(2,1)}, u32[]{:S(2)}, u32[]{:S(2)}) async-start(bf16[128,8,2560]{2,1,0:T(8,128)(2,1)} %pack.1), calls=%async_computation | async-start | bytes 10485760 | tf_op jit(solution)/shard_map/all_to_all | solution.py:298
  20.7 7.5 %collective-permute-start = (f32[4,2560]{1,0:T(4,128)S(1)}, f32[4,2560]{1,0:T(4,128)S(1)}, u32[]{:S(2)}, u32[]{:S(2)}) collective-permute-start(f32[4,2560]{1,0:T(4,128)S(1)} %select_maximum_fusion), channel_id=1, source_target_pairs={{2,0},{4,2},{6,4},{8,6},{10,8},{12,10},{14,12},{16,14},{18,16},{20... | collective-permute-start | bytes 122888 | tf_op jit(solution)/shard_map/ppermute | solution.py:287
  24.5 1.5 %copy-start.1 = (bf16[2,256,2560]{2,1,0:T(8,128)(2,1)}, bf16[2,256,2560]{2,1,0:T(8,128)(2,1)S(1)}, u32[]{:S(2)}) copy-start(bf16[2,256,2560]{2,1,0:T(8,128)(2,1)S(1)} %get-tuple-element.8.dirs) | copy-start | bytes 7864324
  25.9 0.7 copy-start.2
  28.2 110.8 %copy-start.5 = (f32[4,2560]{1,0:T(4,128)}, f32[4,2560]{1,0:T(4,128)S(1)}, u32[]{:S(2)}) copy-start(f32[4,2560]{1,0:T(4,128)S(1)} %collective-permute-done.edge) | copy-start | bytes 122884
